TPU v7x, 256 devices: a whole 4x4x8 slice. The times are simulated.
256 devices in a mesh: seq: 64 (over z, y, core), hid: 4 (over x).
Axes of the slice: x: 4, y: 4, z: 8, core: 2. Of those that a mesh axis runs over, the one named last changes fastest.
Arguments:
- gate_half: bfloat16 [8192, 2048], P('seq', 'hid'), may hold values from -6 to 6
- value_half: bfloat16 [8192, 2048], P('seq', 'hid'), may hold values from -6 to 6
- norm_gain: float32 [2048], P('hid'), may hold values from 0.25 to 1.75
- norm_shift: float32 [2048], P('hid'), may hold values from -0.5 to 0.5
- token_weight: bfloat16 [8192, 8192], P('seq'), may hold values from -0.1875 to 0.1875
- token_bias: float32 [8192], P('seq'), may hold values from 0.5 to 1.5
- grad_output: bfloat16 [8192, 2048], P('seq', 'hid'), may hold values from -6 to 6
Outputs:
- grad_gate: bfloat16 [8192, 2048], P('seq', 'hid')
- grad_value: bfloat16 [8192, 2048], P('seq', 'hid')
- grad_gain: float32 [2048], P('hid')
- grad_shift: float32 [2048], P('hid')
- grad_weight: float32 [8192, 8192], P('seq', 'hid')
- grad_token_bias: float32 [8192], P('seq')
All inputs are finite; a program needn't handle non-finite values.
Results may differ from a plain program's by a relative error of at most 0.005.
Values may be sent and summed in bfloat16 or wider, within the bound.
A program may use at most 64 MiB of HBM per device.

v0:
```python
import jax
import jax.numpy as jnp
from jax import lax
from jax.sharding import PartitionSpec as P

HIDDEN_SIZE = 2048


def sent_to_all(array, axis):
    copies = jnp.broadcast_to(array, (lax.axis_size(axis), *array.shape))
    return lax.all_to_all(copies, axis, split_axis=0, concat_axis=0, tiled=True)


def taken_together(array, axis):
    everything = sent_to_all(array, axis)
    return jnp.sum(everything, axis=0)


def packed_total(arrays, axis):
    flat, at, gathered = (jnp.concatenate([a.reshape(-1) for a in arrays]), 0, [])
    subtotal = taken_together(flat, axis)
    for a in arrays:
        gathered.append(subtotal[at : at + a.size].reshape(a.shape))
        at += a.size
    return tuple(gathered)


def per_device(gate_half, value_half, norm_gain, norm_shift, token_weight, token_bias, grad_output):
    local_rows = gate_half.shape[0]
    channels = gate_half.shape[1]
    all_tokens = token_weight.shape[1]
    row_start = lax.axis_index("seq") * local_rows
    row_last = row_start + local_rows - 1
    row_ids = row_start + lax.iota(jnp.int32, local_rows)[:, None]
    second = value_half.astype(jnp.float32)
    upstream = grad_output.astype(jnp.float32)
    grad_mix = (upstream * gate_half.astype(jnp.float32)).astype(jnp.bfloat16)
    sum_first, sum_square, grad_token_bias = lax.psum(
        (
            jnp.sum(second, axis=1),
            jnp.sum(second * second, axis=1),
            jnp.sum(grad_mix.astype(jnp.float32), axis=1),
        ),
        "hid",
    )
    row_mean = (sum_first / HIDDEN_SIZE)[:, None]
    row_var = (sum_square / HIDDEN_SIZE)[:, None] - row_mean * row_mean
    inv_std = lax.rsqrt(row_var + 1e-05)
    centred = (second - row_mean) * inv_std
    normed = (centred * norm_gain + norm_shift).astype(jnp.bfloat16)
    start_pair = (
        jnp.zeros((local_rows, channels), jnp.float32),
        jnp.zeros((local_rows, all_tokens), jnp.float32),
    )
    shard_rows = lax.all_gather(normed, "seq", axis=0, tiled=True)
    length = shard_rows.shape[0]

    def compute(pair):
        weight_block = token_weight
        column_ids = lax.iota(jnp.int32, length)[None, :]
        lower_mask = column_ids <= row_ids
        weight_block = jnp.where(lower_mask, weight_block, jnp.zeros_like(weight_block))
        mixed_sum = jnp.dot(weight_block, shard_rows, preferred_element_type=jnp.float32)
        outer = jnp.einsum("tc,nc->tn", grad_mix, shard_rows, preferred_element_type=jnp.float32)
        outer = jnp.where(lower_mask, outer, 0.0)
        return (mixed_sum, outer)

    mixed_sum, weight_term = lax.cond(
        jnp.int32(0) <= row_last, compute, lambda pair: pair, start_pair
    )
    spatial = mixed_sum + token_bias[:, None]
    grad_gate = (upstream * spatial).astype(jnp.bfloat16)
    grad_weight = lax.psum_scatter(weight_term, "hid", scatter_dimension=1, tiled=True)
    columns = lax.all_to_all(token_weight, "seq", split_axis=1, concat_axis=0, tiled=True)
    own_ids = row_start + lax.iota(jnp.int32, local_rows)[None, :]
    fold_shard_rows = lax.all_gather(grad_mix, "seq", axis=0, tiled=True)
    fold_length = fold_shard_rows.shape[0]

    def compute(running):
        weight_block = columns
        source_ids = lax.iota(jnp.int32, fold_length)[:, None]
        weight_block = jnp.where(source_ids >= own_ids, weight_block, jnp.zeros_like(weight_block))
        return jnp.einsum(
            "nt,nc->tc", weight_block, fold_shard_rows, preferred_element_type=jnp.float32
        )

    grad_normed = lax.cond(
        jnp.int32(0) + fold_length - 1 >= row_start,
        compute,
        lambda running: running,
        jnp.zeros((local_rows, channels), jnp.float32),
    )
    grad_gain, grad_shift = packed_total(
        (jnp.sum(grad_normed * centred, axis=0), jnp.sum(grad_normed, axis=0)), "seq"
    )
    grad_centred = grad_normed * norm_gain
    sum_grad, sum_cross = lax.psum(
        (jnp.sum(grad_centred, axis=1), jnp.sum(grad_centred * centred, axis=1)), "hid"
    )
    first_mean = (sum_grad / HIDDEN_SIZE)[:, None]
    second_mean = (sum_cross / HIDDEN_SIZE)[:, None]
    grad_value = (inv_std * (grad_centred - first_mean - centred * second_mean)).astype(
        jnp.bfloat16
    )
    return (grad_gate, grad_value, grad_gain, grad_shift, grad_weight, grad_token_bias)


def solution(mesh):
    placed = (
        P("seq", "hid"),
        P("seq", "hid"),
        P("hid"),
        P("hid"),
        P("seq", None),
        P("seq"),
        P("seq", "hid"),
    )
    return jax.shard_map(
        per_device,
        mesh=mesh,
        in_specs=placed,
        out_specs=(P("seq", "hid"), P("seq", "hid"), P("hid"), P("hid"), P("seq", "hid"), P("seq")),
        check_vma=False,
    )
```

profile of v0, /device:TPU:1, one launch (start us, length us, event | category | flops | bytes accessed | tf_op | source)
XLA Modules:
  0.0 270.6 jit_solution(11396971279304036208)
XLA Ops:
  7.2 0.0 all-gather.5.cloned.1.call-start
  7.2 1.7 convert_reduce_fusion.1
  8.9 0.0 all-gather.5.cloned.1.call-update
  8.9 0.0 copy-start.3
  8.9 4.1 %copy.17 = bf16[128,8192]{0,1:T(8,128)(2,1)} copy(bf16[128,8192]{1,0:T(8,128)(2,1)} %param.15) | data formatting | bytes 4194304 | tf_op args[4]
  13.0 13.1 %all-to-all-start = ((bf16[128,64,128]{0,2,1:T(8,128)(2,1)}), bf16[128,64,128]{0,2,1:T(8,128)(2,1)S(1)}, u32[]{:S(2)}, u32[]{:S(2)}) async-start(bf16[128,64,128]{0,2,1:T(8,128)(2,1)} %bitcast.13), calls=%async_computation | async-start | bytes 4194304 | tf_op jit(solution)/shard_map/all_to_all | solution.py:74
  26.2 0.0 all-gather.3.cloned.1.call-start
  26.2 0.1 convert_reduce_fusion
  26.4 9.1 %all-reduce.1 = (f32[128]{0:T(128)S(1)}, f32[128]{0:T(128)S(1)}) all-reduce(f32[128]{0:T(128)S(1)} %get-tuple-element.62, f32[128]{0:T(128)S(1)} %get-tuple-element.61), channel_id=1, replica_groups=mesh['seq'=64,'hid'=4] {'hid'}, use_global_device_ids=true, to_apply=%region_3.0 | all-reduce | flops 256 | bytes 2048 | tf_op jit(solution)/shard_map/psum | solution.py:38
  35.5 48.1 %all-to-all-done = bf16[128,64,128]{0,2,1:T(8,128)(2,1)S(1)} async-done(((bf16[128,64,128]{0,2,1:T(8,128)(2,1)}), bf16[128,64,128]{0,2,1:T(8,128)(2,1)S(1)}, u32[]{:S(2)}, u32[]{:S(2)}) %all-to-all-start) | async-done | bytes 2097184 | tf_op jit(solution)/shard_map/all_to_all | solution.py:74
  83.6 23.1 %all-gather.5.cloned.1.call-done = bf16[8192,512]{1,0:T(8,128)(2,1)} async-done(((bf16[128,512]{1,0:T(8,128)(2,1)}), bf16[8192,512]{1,0:T(8,128)(2,1)}) %all-gather.5.cloned.1.call-update) | async-done | bytes 8388624 | tf_op jit(solution)/shard_map/all_gather | solution.py:76
  106.7 9.3 %conditional.3 = (f32[128,512]{1,0:T(8,128)S(1)}) conditional(s32[]{:T(128)} %convert_element_type.37, () %tuple.24, (s32[]{:T(128)}, s32[1,128]{1,0:T(1,128)S(1)}, bf16[64,128,128]{1,2,0:T(8,128)(2,1)S(1)}, bf16[8192,512]{1,0:T(8,128)(2,1)}) %tuple.49), branch_computations={%region_6.0_spmd, %region_7.8_spmd} | conditional | flops 1075839104 | bytes 23332392 | solution.py:87
  106.7 1.4 copy-done.1
  108.1 3.2 %copy.18 = bf16[64,128,128]{2,1,0:T(8,128)(2,1)S(1)} copy(bf16[64,128,128]{1,2,0:T(8,128)(2,1)} %copy-done.1) | data formatting | bytes 4194304 | tf_op jit(solution)/shard_map
  111.3 4.7 %fusion.7 = f32[128,512]{1,0:T(8,128)S(1)} fusion(bf16[8192,512]{1,0:T(8,128)(2,1)} %get-tuple-element.34, bf16[8192,128]{1,0:T(8,128)(2,1)S(1)} %bitcast.11, s32[128]{0:T(128)S(1)} %add_bitcast_fusion.1), kind=kOutput, calls=%fused_computation.10 | convolution fusion | flops 1075838976 | bytes 10748416 | tf_op jit(solution)/shard_map/cond/branch_1_fun/nt,nc->tc/dot_general | solution.py:83
  116.0 0.2 fusion.25
  116.2 9.0 %all-reduce = (f32[128]{0:T(128)S(1)}, f32[128]{0:T(128)S(1)}, f32[128]{0:T(128)}) all-reduce(f32[128]{0:T(128)S(1)} %get-tuple-element.58, f32[128]{0:T(128)S(1)} %get-tuple-element.59, f32[128]{0:T(128)S(1)} %get-tuple-element.68), channel_id=1, replica_groups=mesh['seq'=64,'hid'=4] {'hid'}, use_global_device_ids=true, to_apply=%region_11.12 | all-reduce | flops 384 | bytes 3072 | tf_op jit(solution)/shard_map/psum | solution.py:97
  125.2 0.9 fusion.24
  126.1 0.0 all-gather.3.cloned.1.call-update
  126.1 0.0 reduce-scatter.2.cloned.1.call-start
  126.2 80.8 %all-gather.3.cloned.1.call-done = bf16[8192,512]{1,0:T(8,128)(2,1)} async-done(((bf16[128,512]{1,0:T(8,128)(2,1)}), bf16[8192,512]{1,0:T(8,128)(2,1)}) %all-gather.3.cloned.1.call-update) | async-done | bytes 8388624 | tf_op jit(solution)/shard_map/all_gather | solution.py:55
  207.0 11.2 %conditional.2 = (f32[128,512]{1,0:T(8,128)S(1)}, f32[128,8192]{1,0:T(8,128)}) conditional(s32[]{:T(128)} %convert_element_type.31, () %tuple.22, (s32[]{:T(128)}, s32[128,1]{0,1:T(1,128)S(1)}, bf16[128,8192]{1,0:T(8,128)(2,1)}, bf16[8192,512]{1,0:T(8,128)(2,1)}, bf16[128,512]{1,0:T(8,128)(2,1)S(1)}) %tuple.50), branch_computations={%region_4.0_spmd, %region_5.0_spmd} | conditional | flops 2151677952 | bytes 57018416 | solution.py:68
  207.0 5.4 %fusion.1 = f32[128,512]{1,0:T(8,128)S(1)} fusion(bf16[8192,512]{1,0:T(8,128)(2,1)} %get-tuple-element.29, bf16[128,8192]{1,0:T(8,128)(2,1)} %get-tuple-element.28, s32[128]{0:T(128)S(1)} %add_bitcast_fusion), kind=kOutput, calls=%fused_computation.3 | convolution fusion | flops 1075838976 | bytes 10748416 | tf_op jit(solution)/shard_map/cond/branch_1_fun/dot_general | solution.py:63
  212.5 0.9 copy-done
  213.4 4.8 %convolution_select_fusion = f32[128,8192]{1,0:T(8,128)} fusion(bf16[128,512]{1,0:T(8,128)(2,1)S(1)} %get-tuple-element.30, bf16[8192,512]{1,0:T(8,128)(2,1)S(1)} %copy-done, s32[128]{0:T(128)S(1)} %add_bitcast_fusion), kind=kOutput, calls=%fused_computation | convolution fusion | flops 1075838976 | bytes 12714496 | tf_op jit(solution)/shard_map/cond/branch_1_fun/tc,nc->tn/dot_general | solution.py:64
  218.2 0.0 reduce-scatter.2.cloned.1.call-update
  218.2 0.1 broadcast_in_dim.8
  218.4 18.7 %all_to_all.25 = f32[64,1,1024]{2,1,0:T(1,128)S(1)} all-to-all(f32[64,1,1024]{2,1,0:T(1,128)S(1)} %broadcast_in_dim.8), channel_id=1, replica_groups=mesh['seq'=64,'hid'=4] {'seq'}, dimensions={0} | all-to-all | bytes 524288 | tf_op jit(solution)/shard_map/all_to_all | solution.py:11
  237.1 0.2 reduce_sum.78
  237.2 0.6 fusion.28
  237.8 0.8 fusion.13
  238.6 25.5 %reduce-scatter.2.cloned.1.call-done = f32[128,2048]{1,0:T(8,128)} async-done(((f32[128,8192]{1,0:T(8,128)}), f32[128,2048]{1,0:T(8,128)}) %reduce-scatter.2.cloned.1.call-update) | async-done | bytes 1048592 | tf_op jit(solution)/shard_map/reduce_scatter | solution.py:73
  (20 shorter events, 0.1 us)
Async XLA Ops:
  7.2 99.5 %all-gather.5.cloned.1.call-start = ((), (), s32[]{:S(2)}) async-start(), calls=%async_computation.4 | async-start | bytes 8519680 | tf_op jit(solution)/shard_map/all_gather | solution.py:76
  8.9 17.3 %copy-start.3 = (bf16[128,512]{1,0:T(8,128)(2,1)S(1)}, bf16[128,512]{1,0:T(8,128)(2,1)}, u32[]{:S(2)}) copy-start(bf16[128,512]{1,0:T(8,128)(2,1)} %param.12) | copy-start | bytes 393220
  13.0 70.6 %all-to-all-start = ((bf16[128,64,128]{0,2,1:T(8,128)(2,1)}), bf16[128,64,128]{0,2,1:T(8,128)(2,1)S(1)}, u32[]{:S(2)}, u32[]{:S(2)}) async-start(bf16[128,64,128]{0,2,1:T(8,128)(2,1)} %bitcast.13), calls=%async_computation | async-start | bytes 4194304 | tf_op jit(solution)/shard_map/all_to_all | solution.py:74
  26.2 180.8 %all-gather.3.cloned.1.call-start = ((), (), s32[]{:S(2)}) async-start(), calls=%async_computation.3 | async-start | bytes 8519680 | tf_op jit(solution)/shard_map/all_gather | solution.py:55
  106.7 9.3 %copy-start.5 = (f32[512]{0:T(512)S(1)}, f32[512]{0:T(512)}, u32[]{:S(2)}) copy-start(f32[512]{0:T(512)} %param.13) | copy-start | bytes 6148
  106.7 18.6 %copy-start.6 = (f32[512]{0:T(512)S(1)}, f32[512]{0:T(512)}, u32[]{:S(2)}) copy-start(f32[512]{0:T(512)} %param.14) | copy-start | bytes 6148
  106.7 100.3 %copy-start.2 = (bf16[128,512]{1,0:T(8,128)(2,1)S(1)}, bf16[128,512]{1,0:T(8,128)(2,1)}, u32[]{:S(2)}) copy-start(bf16[128,512]{1,0:T(8,128)(2,1)} %get-tuple-element.69) | copy-start | bytes 393220
  106.7 1.4 copy-start.1
  126.1 138.0 %reduce-scatter.2.cloned.1.call-start = ((), (), s32[]{:S(2)}) async-start(), calls=%async_computation.5 | async-start | bytes 5242880 | tf_op jit(solution)/shard_map/reduce_scatter | solution.py:73
  207.0 6.4 %copy-start = (bf16[8192,512]{1,0:T(8,128)(2,1)S(1)}, bf16[8192,512]{1,0:T(8,128)(2,1)}, u32[]{:S(2)}) copy-start(bf16[8192,512]{1,0:T(8,128)(2,1)} %get-tuple-element.29) | copy-start | bytes 25165828 | tf_op jit(solution)/shard_map/cond
  218.2 19.6 %copy-start.4 = (bf16[128,512]{1,0:T(8,128)(2,1)S(1)}, bf16[128,512]{1,0:T(8,128)(2,1)}, u32[]{:S(2)}) copy-start(bf16[128,512]{1,0:T(8,128)(2,1)} %param.17) | copy-start | bytes 393220
  218.2 19.6 %copy-start.7 = (f32[128]{0:T(128)S(1)}, f32[128]{0:T(128)}, u32[]{:S(2)}) copy-start(f32[128]{0:T(128)} %param.16) | copy-start | bytes 1540
Sparse Core Ops, SparseCore 0:
  11.3 95.2 all-gather.4
  126.2 80.7 all-gather.2
  218.4 45.6 reduce-scatter.1
where the time goes:
time: 271 us
  waiting for transfers between devices  178 us (66%)
  blocking collectives  36.8 us (14%)
  matrix products  15 us (6%)
  between operations  13.8 us (5%)
  starting transfers between devices  13.3 us (5%)
  local copies, waits for them, and re-layouts  10.4 us (4%)
  other arithmetic  3.82 us (1%)
    all_gather x1, waiting for transfers between devices, per_device(): shard_rows = lax.all_gather(normed, 'seq', axis=0, tiled=True)  80.8 us
    all_to_all x1, waiting for transfers between devices, per_device(): lax.all_to_all(token_weight, 'seq', split_axis=1, concat_axis=0, tiled=True)  48.1 us
    reduce_scatter x1, waiting for transfers between devices, per_device(): lax.psum_scatter(weight_term, 'hid', scatter_dimension=1, tiled=True)  25.5 us
    all_gather x1, waiting for transfers between devices, per_device(): fold_shard_rows = lax.all_gather(grad_mix, 'seq', axis=0, tiled=True)  23.1 us
    all_to_all x1, blocking collectives, sent_to_all(): return lax.all_to_all(copies, axis, split_axis=0, concat_axis=0, tiled=True)  18.7 us
    all_to_all x1, starting transfers between devices, per_device(): lax.all_to_all(token_weight, 'seq', split_axis=1, concat_axis=0, tiled=True)  13.1 us
    psum x1, blocking collectives, per_device(): lax.psum((jnp.sum(second, axis=1), jnp.sum(second * second, axis=1), jnp....  9.12 us
    psum x1, blocking collectives, per_device(): lax.psum((jnp.sum(grad_centred, axis=1), jnp.sum(grad_centred * centred,...  8.99 us
  transfers between devices with their start and end apart: 4, of which 4 were waited for; matrix products, arithmetic and copies ran while one was open for 2% of the time, Pallas kernels for 0%

commit v1 on v0

--- a/solution.py
+++ b/solution.py
@@ -1,9 +1,24 @@
+import functools
 import jax
 import jax.numpy as jnp
 from jax import lax
 from jax.sharding import PartitionSpec as P
 
 HIDDEN_SIZE = 2048
+
+
+def guide_sections(base_x, mesh_ax):
+    dev_count = lax.axis_size(mesh_ax)
+    slots = []
+    for tick in range(base_x.ndim):
+        slots.append(dev_count if tick == 0 else 1)
+    moved = lax.all_to_all(
+        jnp.tile(base_x, slots), mesh_ax, split_axis=0, concat_axis=0, tiled=True
+    )
+    return moved
+
+
+derive_panels_for = functools.partial(guide_sections, mesh_ax="seq")
 
 
 def sent_to_all(array, axis):
@@ -52,7 +67,7 @@
         jnp.zeros((local_rows, channels), jnp.float32),
         jnp.zeros((local_rows, all_tokens), jnp.float32),
     )
-    shard_rows = lax.all_gather(normed, "seq", axis=0, tiled=True)
+    shard_rows = derive_panels_for(normed)
     length = shard_rows.shape[0]
 
     def compute(pair):

time: 271 us -> 390 us (1.44)
  waiting for transfers between devices: 178 us -> 277 us
  starting transfers between devices: 13.3 us -> 22.4 us
  blocking collectives: 36.8 us -> 41.1 us
    all_to_all x0 -> x1, waiting for transfers between devices: none -> 182 us  [guide_sections(): lax.all_to_all(jnp.tile(base_x, slots), mesh_ax, split_axis=0, concat_axi...]
    all_gather x1 -> x0, waiting for transfers between devices: 80.8 us -> none  [per_device(): shard_rows = lax.all_gather(normed, 'seq', axis=0, tiled=True)]
    all_to_all x0 -> x1, starting transfers between devices: none -> 9.17 us  [guide_sections(): lax.all_to_all(jnp.tile(base_x, slots), mesh_ax, split_axis=0, concat_axi...]
    all_to_all x1, blocking collectives: 18.7 us -> 22.9 us  [sent_to_all(): return lax.all_to_all(copies, axis, split_axis=0, concat_axis=0, tiled=True)]
    another operation x1 -> x2, local copies, waits for them, and re-layouts: 3.22 us -> 7.44 us  [the longest x1 4.22 us: guide_sections(): jnp.tile(base_x, slots)]
where the time goes in v1:
time: 390 us
  waiting for transfers between devices  277 us (71%)
  blocking collectives  41.1 us (11%)
  starting transfers between devices  22.4 us (6%)
  matrix products  17.6 us (5%)
  between operations  14.1 us (4%)
  local copies, waits for them, and re-layouts  13.7 us (4%)
    all_to_all x1, waiting for transfers between devices, guide_sections(): lax.all_to_all(jnp.tile(base_x, slots), mesh_ax, split_axis=0, concat_axi...  182 us
    all_to_all x1, waiting for transfers between devices, per_device(): lax.all_to_all(token_weight, 'seq', split_axis=1, concat_axis=0, tiled=True)  47.9 us
    reduce_scatter x1, waiting for transfers between devices, per_device(): lax.psum_scatter(weight_term, 'hid', scatter_dimension=1, tiled=True)  23.4 us
    all_gather x1, waiting for transfers between devices, per_device(): fold_shard_rows = lax.all_gather(grad_mix, 'seq', axis=0, tiled=True)  23.3 us
    all_to_all x1, blocking collectives, sent_to_all(): return lax.all_to_all(copies, axis, split_axis=0, concat_axis=0, tiled=True)  22.9 us
    all_to_all x1, starting transfers between devices, per_device(): lax.all_to_all(token_weight, 'seq', split_axis=1, concat_axis=0, tiled=True)  13.1 us
    all_to_all x1, starting transfers between devices, guide_sections(): lax.all_to_all(jnp.tile(base_x, slots), mesh_ax, split_axis=0, concat_axi...  9.17 us
    psum x1, blocking collectives, per_device(): lax.psum((jnp.sum(second, axis=1), jnp.sum(second * second, axis=1), jnp....  9.17 us
  transfers between devices with their start and end apart: 4, of which 4 were waited for; matrix products, arithmetic and copies ran while one was open for 2% of the time, Pallas kernels for 0%

profile of v1, /device:TPU:1, one launch (start us, length us, event | category | flops | bytes accessed | tf_op | source)
XLA Modules:
  0.0 389.5 jit_solution(18036650060977032159)
XLA Ops:
  7.2 0.0 all-gather.2.cloned.1.call-start
  7.2 1.7 convert_reduce_fusion.1
  8.9 0.0 all-gather.2.cloned.1.call-update
  8.9 0.0 copy-start.3
  8.9 4.1 %copy.17 = bf16[128,8192]{0,1:T(8,128)(2,1)} copy(bf16[128,8192]{1,0:T(8,128)(2,1)} %param.15) | data formatting | bytes 4194304 | tf_op args[4]
  13.0 13.1 %all-to-all-start.1 = ((bf16[128,64,128]{0,2,1:T(8,128)(2,1)}), bf16[128,64,128]{0,2,1:T(8,128)(2,1)S(1)}, u32[]{:S(2)}, u32[]{:S(2)}) async-start(bf16[128,64,128]{0,2,1:T(8,128)(2,1)} %bitcast.14), calls=%async_computation.1 | async-start | bytes 4194304 | tf_op jit(solution)/shard_map/all_to_all | solution.py:89
  26.2 0.1 convert_reduce_fusion
  26.3 9.2 %all-reduce.1 = (f32[128]{0:T(128)S(1)}, f32[128]{0:T(128)S(1)}) all-reduce(f32[128]{0:T(128)S(1)} %get-tuple-element.63, f32[128]{0:T(128)S(1)} %get-tuple-element.62), channel_id=1, replica_groups=mesh['seq'=64,'hid'=4] {'hid'}, use_global_device_ids=true, to_apply=%region_3.0 | all-reduce | flops 256 | bytes 2048 | tf_op jit(solution)/shard_map/psum | solution.py:53
  35.5 47.9 %all-to-all-done.1 = bf16[128,64,128]{0,2,1:T(8,128)(2,1)S(1)} async-done(((bf16[128,64,128]{0,2,1:T(8,128)(2,1)}), bf16[128,64,128]{0,2,1:T(8,128)(2,1)S(1)}, u32[]{:S(2)}, u32[]{:S(2)}) %all-to-all-start.1) | async-done | bytes 2097184 | tf_op jit(solution)/shard_map/all_to_all | solution.py:89
  83.4 23.3 %all-gather.2.cloned.1.call-done = bf16[8192,512]{1,0:T(8,128)(2,1)} async-done(((bf16[128,512]{1,0:T(8,128)(2,1)}), bf16[8192,512]{1,0:T(8,128)(2,1)}) %all-gather.2.cloned.1.call-update) | async-done | bytes 8388624 | tf_op jit(solution)/shard_map/all_gather | solution.py:91
  106.7 9.3 %conditional.3 = (f32[128,512]{1,0:T(8,128)S(1)}) conditional(s32[]{:T(128)} %convert_element_type.37, () %tuple.24, (s32[]{:T(128)}, s32[1,128]{1,0:T(1,128)S(1)}, bf16[64,128,128]{1,2,0:T(8,128)(2,1)S(1)}, bf16[8192,512]{1,0:T(8,128)(2,1)}) %tuple.47), branch_computations={%region_6.0_spmd, %region_7.8_spmd} | conditional | flops 1075839104 | bytes 23332392 | solution.py:102
  106.7 1.4 copy-done
  108.1 3.2 copy.18
  111.3 4.7 %fusion.7 = f32[128,512]{1,0:T(8,128)S(1)} fusion(bf16[8192,512]{1,0:T(8,128)(2,1)} %get-tuple-element.35, bf16[8192,128]{1,0:T(8,128)(2,1)S(1)} %bitcast.12, s32[128]{0:T(128)S(1)} %add_bitcast_fusion.1), kind=kOutput, calls=%fused_computation.10 | convolution fusion | flops 1075838976 | bytes 10748416 | tf_op jit(solution)/shard_map/cond/branch_1_fun/nt,nc->tc/dot_general | solution.py:98
  116.0 0.2 fusion.25
  116.2 9.0 %all-reduce = (f32[128]{0:T(128)S(1)}, f32[128]{0:T(128)S(1)}, f32[128]{0:T(128)}) all-reduce(f32[128]{0:T(128)S(1)} %get-tuple-element.59, f32[128]{0:T(128)S(1)} %get-tuple-element.60, f32[128]{0:T(128)S(1)} %get-tuple-element.69), channel_id=1, replica_groups=mesh['seq'=64,'hid'=4] {'hid'}, use_global_device_ids=true, to_apply=%region_11.12 | all-reduce | flops 384 | bytes 3072 | tf_op jit(solution)/shard_map/psum | solution.py:112
  125.2 0.8 fusion.24
  126.1 4.2 %tile.2 = bf16[64,128,512]{2,1,0:T(8,128)(2,1)} broadcast(bf16[128,512]{1,0:T(8,128)(2,1)S(1)} %get-tuple-element.72), dimensions={1,2} | broadcast | bytes 8519680 | tf_op jit(solution)/shard_map/tile | solution.py:16
  130.3 9.2 %all-to-all-start = ((bf16[64,128,512]{2,1,0:T(8,128)(2,1)}), bf16[64,128,512]{2,1,0:T(8,128)(2,1)}, u32[]{:S(2)}, u32[]{:S(2)}) async-start(bf16[64,128,512]{2,1,0:T(8,128)(2,1)} %tile.2), calls=%async_computation | async-start | bytes 16777216 | tf_op jit(solution)/shard_map/all_to_all | solution.py:15
  139.5 0.0 reduce-scatter.2.cloned.1.call-start
  139.5 182.2 %all-to-all-done = bf16[64,128,512]{2,1,0:T(8,128)(2,1)} async-done(((bf16[64,128,512]{2,1,0:T(8,128)(2,1)}), bf16[64,128,512]{2,1,0:T(8,128)(2,1)}, u32[]{:S(2)}, u32[]{:S(2)}) %all-to-all-start) | async-done | bytes 8388640 | tf_op jit(solution)/shard_map/all_to_all | solution.py:15
  321.8 0.0 copy-done.1
  321.8 12.9 %conditional.2 = (f32[128,512]{1,0:T(8,128)S(1)}, f32[128,8192]{1,0:T(8,128)}) conditional(s32[]{:T(128)} %convert_element_type.31, () %tuple.22, (s32[]{:T(128)}, s32[128,1]{0,1:T(1,128)S(1)}, bf16[128,8192]{1,0:T(8,128)(2,1)S(1)}, bf16[64,128,512]{2,1,0:T(8,128)(2,1)}, bf16[128,512]{1,0:T(8,128)(2,1)S(1)}) %tuple.49), branch_computations={%region_4.0_spmd, %region_5.0_spmd} | conditional | flops 2151677952 | bytes 23463956 | solution.py:83
  321.8 4.7 %fusion.1 = f32[128,512]{1,0:T(8,128)S(1)} fusion(bf16[8192,512]{1,0:T(8,128)(2,1)} %bitcast.1, bf16[128,8192]{1,0:T(8,128)(2,1)S(1)} %get-tuple-element.29, s32[128]{0:T(128)S(1)} %add_bitcast_fusion), kind=kOutput, calls=%fused_computation.3 | convolution fusion | flops 1075838976 | bytes 10748416 | tf_op jit(solution)/shard_map/cond/branch_1_fun/dot_general | solution.py:78
  326.5 8.2 %convolution_select_fusion = f32[128,8192]{1,0:T(8,128)} fusion(bf16[128,512]{1,0:T(8,128)(2,1)S(1)} %get-tuple-element.31, bf16[8192,512]{1,0:T(8,128)(2,1)} %bitcast.1, s32[128]{0:T(128)S(1)} %add_bitcast_fusion), kind=kOutput, calls=%fused_computation | convolution fusion | flops 1075838976 | bytes 12714496 | tf_op jit(solution)/shard_map/cond/branch_1_fun/tc,nc->tn/dot_general | solution.py:79
  334.7 0.0 reduce-scatter.2.cloned.1.call-update
  334.7 0.1 broadcast_in_dim.8
  334.9 22.9 %all_to_all.33 = f32[64,1,1024]{2,1,0:T(1,128)S(1)} all-to-all(f32[64,1,1024]{2,1,0:T(1,128)S(1)} %broadcast_in_dim.8), channel_id=1, replica_groups=mesh['seq'=64,'hid'=4] {'seq'}, dimensions={0} | all-to-all | bytes 524288 | tf_op jit(solution)/shard_map/all_to_all | solution.py:26
  357.8 0.2 reduce_sum.78
  358.0 0.6 fusion.28
  358.6 0.8 fusion.13
  359.3 23.4 %reduce-scatter.2.cloned.1.call-done = f32[128,2048]{1,0:T(8,128)} async-done(((f32[128,8192]{1,0:T(8,128)}), f32[128,2048]{1,0:T(8,128)}) %reduce-scatter.2.cloned.1.call-update) | async-done | bytes 1048592 | tf_op jit(solution)/shard_map/reduce_scatter | solution.py:88
  (20 shorter events, 0.1 us)
Async XLA Ops:
  7.2 99.5 %all-gather.2.cloned.1.call-start = ((), (), s32[]{:S(2)}) async-start(), calls=%async_computation.4 | async-start | bytes 8519680 | tf_op jit(solution)/shard_map/all_gather | solution.py:91
  8.9 17.3 %copy-start.3 = (bf16[128,512]{1,0:T(8,128)(2,1)S(1)}, bf16[128,512]{1,0:T(8,128)(2,1)}, u32[]{:S(2)}) copy-start(bf16[128,512]{1,0:T(8,128)(2,1)} %param.12) | copy-start | bytes 393220
  13.0 70.4 %all-to-all-start.1 = ((bf16[128,64,128]{0,2,1:T(8,128)(2,1)}), bf16[128,64,128]{0,2,1:T(8,128)(2,1)S(1)}, u32[]{:S(2)}, u32[]{:S(2)}) async-start(bf16[128,64,128]{0,2,1:T(8,128)(2,1)} %bitcast.14), calls=%async_computation.1 | async-start | bytes 4194304 | tf_op jit(solution)/shard_map/all_to_all | solution.py:89
  106.7 9.3 %copy-start.5 = (f32[512]{0:T(512)S(1)}, f32[512]{0:T(512)}, u32[]{:S(2)}) copy-start(f32[512]{0:T(512)} %param.13) | copy-start | bytes 6148
  106.7 18.6 %copy-start.6 = (f32[512]{0:T(512)S(1)}, f32[512]{0:T(512)}, u32[]{:S(2)}) copy-start(f32[512]{0:T(512)} %param.14) | copy-start | bytes 6148
  106.7 1.4 copy-start
  130.3 191.5 %copy-start.1 = (bf16[128,8192]{1,0:T(8,128)(2,1)S(1)}, bf16[128,8192]{1,0:T(8,128)(2,1)}, u32[]{:S(2)}) copy-start(bf16[128,8192]{1,0:T(8,128)(2,1)} %param.15) | copy-start | bytes 6291460
  130.3 191.5 %copy-start.2 = (bf16[128,512]{1,0:T(8,128)(2,1)S(1)}, bf16[128,512]{1,0:T(8,128)(2,1)}, u32[]{:S(2)}) copy-start(bf16[128,512]{1,0:T(8,128)(2,1)} %get-tuple-element.70) | copy-start | bytes 393220
  130.3 191.5 %all-to-all-start = ((bf16[64,128,512]{2,1,0:T(8,128)(2,1)}), bf16[64,128,512]{2,1,0:T(8,128)(2,1)}, u32[]{:S(2)}, u32[]{:S(2)}) async-start(bf16[64,128,512]{2,1,0:T(8,128)(2,1)} %tile.2), calls=%async_computation | async-start | bytes 16777216 | tf_op jit(solution)/shard_map/all_to_all | solution.py:15
  139.5 243.2 %reduce-scatter.2.cloned.1.call-start = ((), (), s32[]{:S(2)}) async-start(), calls=%async_computation.5 | async-start | bytes 5242880 | tf_op jit(solution)/shard_map/reduce_scatter | solution.py:88
  334.7 23.9 %copy-start.4 = (bf16[128,512]{1,0:T(8,128)(2,1)S(1)}, bf16[128,512]{1,0:T(8,128)(2,1)}, u32[]{:S(2)}) copy-start(bf16[128,512]{1,0:T(8,128)(2,1)} %param.17) | copy-start | bytes 393220
  334.7 23.9 %copy-start.7 = (f32[128]{0:T(128)S(1)}, f32[128]{0:T(128)}, u32[]{:S(2)}) copy-start(f32[128]{0:T(128)} %param.16) | copy-start | bytes 1540
Sparse Core Ops, SparseCore 0:
  11.3 95.3 all-gather.1
  334.8 47.8 reduce-scatter.1
